TPU v7x, 32 devices: a whole 2x2x4 slice. The times are simulated.
32 devices in a mesh: row: 4 (over x, core), col: 8 (over z, y).
Axes of the slice: x: 2, y: 2, z: 4, core: 2. Of those that a mesh axis runs over, the one named last changes fastest.
Arguments:
- tensor: float32 [1024, 32, 1024], P(None, 'row', 'col'), may hold values from -60 to 60, as said below
- factor_two: float32 [32, 32], P('row'), may hold values from -1 to 1
- factor_three: float32 [32, 32], P('col'), may hold values from -1 to 1
- factor_four: float32 [32, 16], replicated, may hold values from -1 to 1
- factor_init: float32 [1024, 64], replicated, may hold values from -6 to 6
Outputs:
- factor_new: float32 [1024, 64], replicated
- core: float32 [64, 32, 32, 16], P(None, 'row', 'col')
Inputs may be any that keep to these rules, and one draw needn't show every extreme that they name: `tensor`: scales vary from slab to slab.
All inputs are finite; a program needn't handle non-finite values.
Results may differ from a plain program's by a relative error of at most 0.00013.
Values sent between devices are 32-bit elements; how exact they have to be, the bound alone decides.
A program may use at most 128 MiB of HBM per device.

v0:
```python
import jax
import jax.numpy as jnp
from jax import lax
from jax.sharding import PartitionSpec as P


def shards(tensor, factor_two, factor_three, factor_four, factor_init):
    highest = lax.Precision.HIGHEST
    first_len = tensor.shape[0]
    local_two = tensor.shape[1]
    fourth_len = factor_four.shape[0]
    local_three = tensor.shape[2] // fourth_len
    rank_one = factor_init.shape[1]
    data = tensor.reshape(first_len, local_two, local_three, fourth_len)
    fourth = jnp.einsum("abcd,de->abce", data, factor_four, precision=highest)
    whole_two = lax.all_gather(factor_two, "row", axis=0, tiled=True)
    spread_two = lax.all_to_all(fourth, "row", split_axis=0, concat_axis=1, tiled=True)
    projected_two = jnp.einsum("abce,bg->agce", spread_two, whole_two, precision=highest)
    partial_two = lax.all_to_all(projected_two, "row", split_axis=1, concat_axis=0, tiled=True)
    whole_three = lax.all_gather(factor_three, "col", axis=0, tiled=True)
    spread_three = lax.all_to_all(partial_two, "col", split_axis=0, concat_axis=2, tiled=True)
    projected_three = jnp.einsum("agce,cf->agfe", spread_three, whole_three, precision=highest)
    block = lax.all_to_all(projected_three, "col", split_axis=2, concat_axis=0, tiled=True)
    columns = block.reshape(first_len, -1)
    basis = factor_init
    local_gram = jnp.dot(columns, columns.T, precision=highest, preferred_element_type=jnp.float32)
    gram = lax.psum(local_gram, ("row", "col"))
    image = jnp.dot(gram, basis, precision=highest, preferred_element_type=jnp.float32)
    square = jnp.dot(image.T, image, precision=highest, preferred_element_type=jnp.float32)
    lower = jnp.linalg.cholesky(square)
    basis = jax.scipy.linalg.solve_triangular(lower, image.T, lower=True).T
    core = jnp.dot(basis.T, columns, precision=highest, preferred_element_type=jnp.float32)
    return (basis, core.reshape(rank_one, block.shape[1], block.shape[2], block.shape[3]))


def solution(mesh):
    in_specs = (P(None, "row", "col"), P("row", None), P("col", None), P(), P())
    out_specs = (P(), P(None, "row", "col", None))
    return jax.shard_map(shards, mesh=mesh, in_specs=in_specs, out_specs=out_specs, check_vma=False)
```

profile of v0, /device:TPU:0, one launch (start us, length us, event | category | flops | bytes accessed | tf_op | source)
XLA Modules:
  0.0 512.5 jit_solution(1816454857235836736)
XLA Ops:
  7.2 0.0 copy-start
  7.2 0.0 copy-start.4
  7.2 5.5 %copy.18 = f32[1024,8,128]{0,2,1:T(8,128)} copy(f32[1024,8,128]{2,1,0:T(8,128)} %param.5) | data formatting | bytes 8388608 | tf_op args[0]
  12.6 0.0 copy-done.4
  12.6 4.2 fusion.12
  16.8 12.2 %copy.19 = f32[1024,8,4,16]{3,2,1,0:T(4,128)} copy(f32[1024,8,4,16]{0,3,2,1:T(8,128)S(1)} %fusion.12) | data formatting | bytes 4194304 | tf_op jit(solution)/shard_map/abcd,de->abce/dot_general | solution.py:15
  29.0 15.5 %reshape.31 = f32[4,1,131072]{2,1,0:T(1,128)} reshape(f32[1024,8,4,16]{3,2,1,0:T(4,128)} %copy.19) | data formatting | bytes 4194304
  44.5 4.4 all-to-all-start
  48.9 0.0 copy-done.5
  48.9 26.7 %all_gather.6 = f32[32,32]{1,0:T(8,128)S(1)} all-gather(f32[8,32]{1,0:T(8,128)S(1)} %copy-done.5), channel_id=1, replica_groups=mesh['row'=4,'col'=8] {'row'}, dimensions={0}, use_global_device_ids=true | all-gather | bytes 5120 | tf_op jit(solution)/shard_map/all_gather | solution.py:16
  75.5 0.0 all-to-all-done
  75.5 1.4 copy-done.2
  76.9 0.5 broadcast.53
  77.4 7.7 %reduce.6 = f32[4,131072]{1,0:T(4,128)S(1)} reduce(f32[4,1,131072]{2,1,0:T(1,128)} %copy-done.2, f32[]{:T(128)} %broadcast.53), dimensions={1}, to_apply=%all_to_all.50.reduce_sub_computation | reduce | bytes 4194308 | tf_op jit(solution)/shard_map/all_to_all | solution.py:17
  85.1 17.9 %reshape.32 = f32[1024,8,4,16]{3,2,1,0:T(4,128)} reshape(f32[4,131072]{1,0:T(4,128)S(1)} %reduce.6) | data formatting | bytes 4194304
  103.0 12.2 %copy.20 = f32[4,256,8,4,16]{1,2,0,4,3:T(8,128)S(1)} copy(f32[4,256,8,4,16]{4,3,2,1,0:T(4,128)} %bitcast.72) | data formatting | bytes 4194304 | tf_op jit(solution)/shard_map/all_to_all | solution.py:17
  115.3 1.9 fusion.2
  117.2 1.2 copy.21
  118.4 28.1 %all_to_all.69 = f32[256,32,4,16]{0,3,2,1:T(8,128)S(1)} all-to-all(f32[256,32,4,16]{0,3,2,1:T(8,128)S(1)} %copy.21), channel_id=1, replica_groups=mesh['row'=4,'col'=8] {'row'}, dimensions={1} | all-to-all | bytes 4194304 | tf_op jit(solution)/shard_map/all_to_all | solution.py:19
  146.6 12.1 %copy.37 = f32[256,4,8,4,16]{4,3,2,0,1:T(4,128)} copy(f32[256,4,8,4,16]{0,4,3,2,1:T(8,128)S(1)} %bitcast.78) | data formatting | bytes 4194304 | tf_op jit(solution)/shard_map/all_to_all | solution.py:19
  158.6 15.4 %reshape.33 = f32[8,1,65536]{2,1,0:T(1,128)} reshape(f32[1024,8,4,16]{3,2,1,0:T(4,128)} %bitcast.73) | data formatting | bytes 4194304
  174.0 6.8 %all-to-all-start.2 = ((f32[8,1,65536]{2,1,0:T(1,128)}), f32[8,1,65536]{2,1,0:T(1,128)}, u32[]{:S(2)}, u32[]{:S(2)}) async-start(f32[8,1,65536]{2,1,0:T(1,128)} %reshape.33), calls=%async_computation.2 | async-start | bytes 4194304 | tf_op jit(solution)/shard_map/all_to_all | solution.py:21
  180.8 0.0 all-reduce.2.cloned.1.call-start
  180.9 0.0 copy-done.6
  180.9 66.5 %all-gather = f32[8,4,32]{2,1,0:T(4,128)S(1)} all-gather(f32[1,4,32]{2,1,0:T(4,128)S(1)} %bitcast.85), channel_id=1, replica_groups=mesh['row'=4,'col'=8] {'col'}, dimensions={0}, use_global_device_ids=true | all-gather | bytes 4608 | tf_op jit(solution)/shard_map/all_gather | solution.py:20
  247.3 0.0 all-to-all-done.2
  247.3 7.2 %reduce.7 = f32[8,65536]{1,0:T(8,128)S(1)} reduce(f32[8,1,65536]{2,1,0:T(1,128)} %all-to-all-done.2, f32[]{:T(128)} %broadcast.53), dimensions={1}, to_apply=%all_to_all.58.reduce_sub_computation | reduce | bytes 4194308 | tf_op jit(solution)/shard_map/all_to_all | solution.py:21
  254.6 17.3 %reshape.34 = f32[1024,8,4,16]{3,2,1,0:T(4,128)} reshape(f32[8,65536]{1,0:T(8,128)S(1)} %reduce.7) | data formatting | bytes 4194304
  271.9 9.8 %copy.35 = f32[8,128,8,4,16]{1,0,4,3,2:T(8,128)S(1)} copy(f32[8,128,8,4,16]{4,3,2,1,0:T(4,128)} %bitcast.74) | data formatting | bytes 4194304 | tf_op jit(solution)/shard_map/all_to_all | solution.py:21
  281.7 1.4 copy.25
  283.1 1.9 convolution_bitcast_fusion
  285.0 1.2 copy.27
  286.2 46.2 %all_to_all.70 = f32[128,8,32,16]{0,3,1,2:T(8,128)S(1)} all-to-all(f32[128,8,32,16]{0,3,1,2:T(8,128)S(1)} %copy.27), channel_id=1, replica_groups=mesh['row'=4,'col'=8] {'col'}, dimensions={2} | all-to-all | bytes 4194304 | tf_op jit(solution)/shard_map/all_to_all | solution.py:23
  332.5 1.2 copy.28
  333.7 8.9 %fusion.14 = f32[1024,1024]{1,0:T(8,128)} fusion(f32[64,8,8,128]{3,2,1,0:T(8,128)S(1)} %bitcast.75), kind=kOutput, calls=%fused_computation.20 | convolution fusion | flops 6442450944 | bytes 6291456 | tf_op jit(solution)/shard_map/dot_general | solution.py:26
  342.6 0.0 all-reduce.2.cloned.1.call-update
  342.7 1.9 copy.41
  344.5 138.8 %all-reduce.2.cloned.1.call-done = f32[1024,1024]{1,0:T(8,128)} async-done(((f32[1024,1024]{1,0:T(8,128)}), f32[1024,1024]{1,0:T(8,128)}) %all-reduce.2.cloned.1.call-update) | async-done | bytes 4194320 | tf_op jit(solution)/shard_map/psum | solution.py:27
  483.4 6.3 %fusion.15 = f32[1024,64]{0,1:T(8,128)S(1)} fusion(f32[1024,1024]{1,0:T(8,128)} %all-reduce.2.cloned.1.call-done, f32[1024,64]{0,1:T(8,128)S(1)} %copy-done), kind=kOutput, calls=%fused_computation.21 | convolution fusion | flops 805306368 | bytes 4718592 | tf_op jit(solution)/shard_map/dot_general | solution.py:28
  489.7 0.4 fusion.16
  490.1 0.1 copy.29
  490.2 5.8 %cholesky.16 = f32[64,64]{1,0:T(8,128)S(1)} custom-call(f32[64,64]{1,0:T(8,128)S(1)} %fusion.10), custom_call_target="Cholesky" | custom-call | tf_op jit(solution)/shard_map/jit(cholesky)/cholesky | solution.py:30
  496.0 0.6 compare_reduce_fusion
  496.7 0.7 fusion.7
  497.3 4.9 custom-call.7
  502.2 0.4 fusion.8
  502.7 0.0 copy-start.3
  502.7 2.5 fusion.5
  (9 shorter events, 0.1 us)
Async XLA Ops:
  7.2 476.2 %copy-start = (f32[1024,64]{0,1:T(8,128)S(1)}, f32[1024,64]{0,1:T(8,128)}, u32[]{:S(2)}) copy-start(f32[1024,64]{0,1:T(8,128)} %param.9) | copy-start | bytes 786436
  7.2 5.5 %copy-start.4 = (f32[32,16]{0,1:T(8,128)S(1)}, f32[32,16]{0,1:T(8,128)}, u32[]{:S(2)}) copy-start(f32[32,16]{0,1:T(8,128)} %param.8) | copy-start | bytes 6148
  44.5 4.4 copy-start.5
  44.5 31.1 %all-to-all-start = ((f32[4,1,131072]{2,1,0:T(1,128)}), f32[4,1,131072]{2,1,0:T(1,128)S(1)}, u32[]{:S(2)}, u32[]{:S(2)}) async-start(f32[4,1,131072]{2,1,0:T(1,128)} %reshape.31), calls=%async_computation | async-start | bytes 4194304 | tf_op jit(solution)/shard_map/all_to_all | solution.py:17
  75.5 1.4 copy-start.2
  174.0 6.8 %copy-start.6 = (f32[4,32]{1,0:T(4,128)S(1)}, f32[4,32]{1,0:T(4,128)}, u32[]{:S(2)}) copy-start(f32[4,32]{1,0:T(4,128)} %param.7) | copy-start | bytes 1540
  174.0 73.3 %all-to-all-start.2 = ((f32[8,1,65536]{2,1,0:T(1,128)}), f32[8,1,65536]{2,1,0:T(1,128)}, u32[]{:S(2)}, u32[]{:S(2)}) async-start(f32[8,1,65536]{2,1,0:T(1,128)} %reshape.33), calls=%async_computation.2 | async-start | bytes 4194304 | tf_op jit(solution)/shard_map/all_to_all | solution.py:21
  180.8 302.5 %all-reduce.2.cloned.1.call-start = ((), (), s32[]{:S(2)}) async-start(), calls=%async_computation.4 | async-start | bytes 8388608 | tf_op jit(solution)/shard_map/psum | solution.py:27
  344.5 158.2 %copy-start.1 = (f32[64,8,8,128]{3,1,2,0:T(8,128)S(1)}, f32[64,8,8,128]{3,1,2,0:T(8,128)}, u32[]{:S(2)}) copy-start(f32[64,8,8,128]{3,1,2,0:T(8,128)} %copy.41) | copy-start | bytes 6291460
  502.7 2.5 copy-start.3
Sparse Core Ops, SparseCore 0:
  342.8 140.5 all-reduce.1
where the time goes:
time: 518 us; the launch traced here: 512 us
  blocking collectives  168 us (32%)
  waiting for transfers between devices  139 us (27%)
  local copies, waits for them, and re-layouts  127 us (25%)
  other arithmetic  27 us (5%)
  matrix products  26.5 us (5%)
  between operations  14.6 us (3%)
  starting transfers between devices  11.2 us (2%)
    psum x1, waiting for transfers between devices, shards(): gram = lax.psum(local_gram, ('row', 'col'))  139 us
    unnamed x20, local copies, waits for them, and re-layouts  74.8 us
    all_gather x1, blocking collectives, shards(): whole_three = lax.all_gather(factor_three, 'col', axis=0, tiled=True)  66.5 us
    all_to_all x1, blocking collectives, shards(): lax.all_to_all(projected_three, 'col', split_axis=2, concat_axis=0, tiled...  46.2 us
    all_to_all x1, blocking collectives, shards(): lax.all_to_all(projected_two, 'row', split_axis=1, concat_axis=0, tiled=T...  28.1 us
    all_gather x1, blocking collectives, shards(): whole_two = lax.all_gather(factor_two, 'row', axis=0, tiled=True)  26.7 us
    all_to_all x2, local copies, waits for them, and re-layouts, shards(): lax.all_to_all(fourth, 'row', split_axis=0, concat_axis=1, tiled=True)  12.7 us
    dot_general x1, local copies, waits for them, and re-layouts, shards(): fourth = jnp.einsum('abcd,de->abce', data, factor_four, precision=highest)  12.2 us
  transfers between devices with their start and end apart: 3, of which 1 were waited for; matrix products, arithmetic and copies ran while one was open for 0% of the time, Pallas kernels for 0%

commit v1 on v0

v1 whole, which is shorter than its diff:
```python
import jax
import jax.numpy as jnp
from jax import lax
from jax.experimental import pallas as pl
from jax.experimental.pallas import tpu as pltpu
from jax.sharding import PartitionSpec as P

HIGHEST = lax.Precision.HIGHEST


def dot(a, b, dims):
    return lax.dot_general(a, b, (dims, ((), ())), precision=HIGHEST, preferred_element_type=jnp.float32)


def inverse_factor(square):
    size = square.shape[0]
    rows = lax.broadcasted_iota(jnp.int32, (size, size), 0)
    cols = lax.broadcasted_iota(jnp.int32, (size, size), 1)
    index = lax.broadcasted_iota(jnp.int32, (size, 1), 0)
    left = square
    right = jnp.where(rows == cols, 1.0, 0.0).astype(jnp.float32)
    for k in range(size):
        scale = lax.rsqrt(left[k:k + 1, k:k + 1])
        column = left[:, k:k + 1] * scale
        pivot_left = left[k:k + 1, :] * scale
        pivot_right = right[k:k + 1, :] * scale
        factor = jnp.where(index > k, column, 0.0)
        left = left - factor * pivot_left
        right = jnp.where(index == k, pivot_right, right - factor * pivot_right)
    return right


def finish_kernel(image_ref, basis_ref, inverse_ref):
    image = image_ref[...]
    inverse = inverse_factor(dot(image, image, ((0,), (0,))))
    inverse_ref[...] = inverse
    basis_ref[...] = dot(image, inverse, ((1,), (1,)))


def finish(image):
    rank = image.shape[1]
    return pl.pallas_call(
        finish_kernel,
        out_shape=(
            jax.ShapeDtypeStruct(image.shape, jnp.float32),
            jax.ShapeDtypeStruct((rank, rank), jnp.float32),
        ),
    )(image)


def shards(tensor, factor_two, factor_three, factor_four, factor_init):
    axes = ("row", "col")
    first_len, local_two, width = tensor.shape
    fourth_len, rank_four = factor_four.shape
    local_three = width // fourth_len
    rank_one = factor_init.shape[1]
    rows, cols = lax.axis_size("row"), lax.axis_size("col")
    devices = rows * cols
    local_pairs = local_two * local_three
    features = rank_four * rank_one
    part = features // devices
    data = tensor.reshape(first_len, local_pairs, fourth_len)
    whole_two = lax.all_gather(factor_two, "row", axis=0, tiled=True)
    whole_three = lax.all_gather(factor_three, "col", axis=0, tiled=True)
    whole_two_len, rank_two = whole_two.shape
    whole_three_len, rank_three = whole_three.shape

    def pull(vectors):
        mixed = jnp.einsum("apd,ar->prd", data, vectors, precision=HIGHEST)
        return jnp.einsum("prd,de->per", mixed, factor_four, precision=HIGHEST).reshape(local_pairs, features)

    def spread(block):
        got = lax.all_to_all(block.reshape(local_pairs, devices, part).transpose(1, 0, 2), axes, 0, 0, tiled=True)
        got = got.reshape(rows, cols, local_two, local_three, part)
        return got.transpose(0, 2, 1, 3, 4).reshape(rows * local_two, cols * local_three, part)

    def gather(block):
        two, three, _ = block.shape
        put = block.reshape(rows, two // rows, cols, three // cols, part).transpose(0, 2, 1, 3, 4)
        put = put.reshape(devices, (two // rows) * (three // cols), part)
        got = lax.all_to_all(put, axes, 0, 0, tiled=True)
        return got.transpose(1, 0, 2).reshape(got.shape[1], features)

    block = spread(pull(factor_init))
    block = jnp.einsum("bcq,bg->gcq", block, whole_two, precision=HIGHEST)
    block = jnp.einsum("gcq,cf->gfq", block, whole_three, precision=HIGHEST)
    block = jnp.einsum("gfq,cf->gcq", block, whole_three, precision=HIGHEST)
    block = jnp.einsum("gcq,bg->bcq", block, whole_two, precision=HIGHEST)
    block = gather(block).reshape(local_pairs, rank_four, rank_one)
    block = jnp.einsum("per,de->pdr", block, factor_four, precision=HIGHEST)
    image = lax.psum(dot(tensor.reshape(first_len, -1), block.reshape(-1, rank_one), ((1,), (0,))), axes)
    basis, inverse = finish(image)
    block = spread(pull(image))
    block = jnp.einsum("bcq,bg->gcq", block, whole_two, precision=HIGHEST)
    block = jnp.einsum("gcq,cf->gfq", block, whole_three, precision=HIGHEST)
    block = gather(block).reshape(-1, rank_four, rank_one)
    core = jnp.einsum("per,sr->spe", block, inverse, precision=HIGHEST)
    return (basis, core.reshape(rank_one, rank_two // rows, rank_three // cols, rank_four))


def solution(mesh):
    in_specs = (P(None, "row", "col"), P("row", None), P("col", None), P(), P())
    out_specs = (P(), P(None, "row", "col", None))
    return jax.shard_map(shards, mesh=mesh, in_specs=in_specs, out_specs=out_specs, check_vma=False)
```

time: 518 us -> 260 us (0.50); the launches traced: 512 us -> 260 us
  blocking collectives: 168 us -> 54.5 us
  local copies, waits for them, and re-layouts: 127 us -> 17.5 us
  other arithmetic: 27 us -> 3.75 us
  waiting for transfers between devices: 139 us -> 127 us
  Pallas kernels: 0 us -> 8.18 us
    unnamed x20 -> x18, local copies, waits for them, and re-layouts: 74.8 us -> 10.4 us
    all_to_all x2, blocking collectives: 74.4 us -> 22.8 us  [the longest x1 11.6 us: gather(): got = lax.all_to_all(put, axes, 0, 0, tiled=True)]
    all_gather x1, blocking collectives: 66.5 us -> 26.5 us  [shards(): whole_three = lax.all_gather(factor_three, 'col', axis=0, tiled=True)]
    all_to_all x6 -> x3, local copies, waits for them, and re-layouts: 37.2 us -> 1.16 us  [spread(): lax.all_to_all(block.reshape(local_pairs, devices, part).transpose(1, 0,...]
    all_gather x1, blocking collectives: 26.7 us -> 5.21 us  [shards(): whole_two = lax.all_gather(factor_two, 'row', axis=0, tiled=True)]
    dot_general x7 -> x11, matrix products: 26.1 us -> 13.9 us  [the longest x1 6.42 us: dot(): lax.dot_general(a, b, (dims, ((), ())), precision=HIGHEST, preferred_elem...]
    another operation x5 -> x0, other arithmetic: 12.1 us -> none  [the longest x3 6.52 us: shards(): lower = jnp.linalg.cholesky(square)]
    psum x1, waiting for transfers between devices: 139 us -> 127 us  [shards(): lax.psum(dot(tensor.reshape(first_len, -1), block.reshape(-1, rank_one),...]
  transfers between devices with their start and end apart: 3 -> 3, of which waited for: 1 -> 1; matrix products, arithmetic and copies ran while one was open for 0% -> 1% of each run, Pallas kernels for 0% -> 3%
where the time goes in v1:
time: 260 us
  waiting for transfers between devices  127 us (49%)
  blocking collectives  54.5 us (21%)
  matrix products  24.4 us (9%)
  local copies, waits for them, and re-layouts  17.5 us (7%)
  between operations  14.4 us (6%)
  starting transfers between devices  9.95 us (4%)
  Pallas kernels  8.18 us (3%)
  other arithmetic  3.75 us (1%)
    psum x1, waiting for transfers between devices, shards(): lax.psum(dot(tensor.reshape(first_len, -1), block.reshape(-1, rank_one),...  127 us
    all_gather x1, blocking collectives, shards(): whole_three = lax.all_gather(factor_three, 'col', axis=0, tiled=True)  26.5 us
    all_to_all x1, blocking collectives, gather(): got = lax.all_to_all(put, axes, 0, 0, tiled=True)  11.6 us
    all_to_all x1, blocking collectives, spread(): lax.all_to_all(block.reshape(local_pairs, devices, part).transpose(1, 0,...  11.3 us
    unnamed x2, matrix products  10.5 us
    unnamed x18, local copies, waits for them, and re-layouts  10.4 us
    pallas_call x1, Pallas kernels, finish(): pl.pallas_call(finish_kernel, out_shape=(jax.ShapeDtypeStruct(image.shape...  8.18 us
    all_to_all x1, starting transfers between devices, spread(): lax.all_to_all(block.reshape(local_pairs, devices, part).transpose(1, 0,...  7.33 us
  transfers between devices with their start and end apart: 3, of which 1 were waited for; matrix products, arithmetic and copies ran while one was open for 1% of the time, Pallas kernels for 3%

profile of v1, /device:TPU:0, one launch (start us, length us, event | category | flops | bytes accessed | tf_op | source)
XLA Modules:
  0.0 259.7 jit_solution(10844368934268274448)
XLA Ops:
  7.2 5.5 %copy.30 = f32[1024,8,128]{0,2,1:T(8,128)} copy(f32[1024,8,128]{2,1,0:T(8,128)} %param.5) | data formatting | bytes 8388608 | tf_op args[0]
  12.7 5.2 %fusion.15 = f32[64,1024]{0,1:S(1)} fusion(f32[1024,64]{0,1:T(8,128)S(1)} %copy-done, f32[1024,1024]{0,1:T(8,128)} %bitcast.102), kind=kOutput, calls=%fused_computation.23 | convolution fusion | flops 805306368 | bytes 4718592
  17.9 0.4 convolution_bitcast_fusion.7
  18.4 0.3 copy.66
  18.8 0.9 reshape.61
  19.7 7.3 %all-to-all-start = ((f32[32,1,1024]{2,1,0:T(1,128)}), f32[32,1,1024]{2,1,0:T(1,128)S(1)}, u32[]{:S(2)}, u32[]{:S(2)}) async-start(f32[32,1,1024]{2,1,0:T(1,128)} %reshape.61), calls=%async_computation | async-start | bytes 262144 | tf_op jit(solution)/shard_map/all_to_all | solution.py:73
  27.1 5.2 %all_gather.6 = f32[32,32]{1,0:T(8,128)S(1)} all-gather(f32[8,32]{1,0:T(8,128)S(1)} %copy-done.2), channel_id=1, replica_groups=mesh['row'=4,'col'=8] {'row'}, dimensions={0}, use_global_device_ids=true | all-gather | bytes 5120 | tf_op jit(solution)/shard_map/all_gather | solution.py:63
  32.3 26.5 %all-gather = f32[8,4,32]{2,1,0:T(4,128)S(1)} all-gather(f32[1,4,32]{2,1,0:T(4,128)S(1)} %bitcast.123), channel_id=1, replica_groups=mesh['row'=4,'col'=8] {'col'}, dimensions={0}, use_global_device_ids=true | all-gather | bytes 4608 | tf_op jit(solution)/shard_map/all_gather | solution.py:64
  58.7 0.5 broadcast
  59.3 0.9 reduce
  60.4 0.3 copy.32
  60.7 0.3 copy.33
  61.0 1.0 convolution_bitcast_fusion.5
  62.0 0.6 copy.35
  62.6 0.6 convolution_bitcast_fusion.4
  63.2 0.6 convolution_bitcast_fusion.3
  63.7 0.6 copy.36
  64.3 0.6 convolution_bitcast_fusion.2
  65.1 0.3 copy.38
  65.4 0.3 copy.39
  65.7 0.3 reshape.63
  66.0 11.6 %all_to_all.20 = f32[32,1,1024]{2,1,0:T(1,128)S(1)} all-to-all(f32[32,1,1024]{2,1,0:T(1,128)S(1)} %reshape.63), channel_id=1, replica_groups=mesh['row'=4,'col'=8] {'row','col'}, dimensions={0} | all-to-all | bytes 262144 | tf_op jit(solution)/shard_map/all_to_all | solution.py:81
  77.5 0.9 reduce.1
  78.7 0.3 copy.40
  79.1 0.6 fusion.12
  79.7 6.4 %fusion.3 = f32[1024,64]{1,0:T(8,128)} fusion(f32[1024,64]{1,0:T(8,128)S(1)} %bitcast.105, f32[128,8,8,128]{3,2,1,0:T(8,128)} %bitcast.104), kind=kOutput, calls=%fused_computation.9 | convolution fusion | flops 805306368 | bytes 4718592 | tf_op jit(solution)/shard_map/dot_general | solution.py:12
  86.2 127.0 %all-reduce.2.cloned.1.call-done.image_ref = f32[1024,64]{1,0:T(8,128)} async-done(((f32[1024,64]{1,0:T(8,128)}), f32[1024,64]{1,0:T(8,128)}) %all-reduce.2.cloned.1.call-update) | async-done | bytes 262160 | tf_op jit(solution)/shard_map/psum | solution.py:91
  213.2 5.3 %fusion.16 = f32[64,1024]{0,1:S(1)} fusion(f32[1024,64]{1,0:T(8,128)} %all-reduce.2.cloned.1.call-done.image_ref, f32[1024,1024]{0,1:T(8,128)} %bitcast.103), kind=kOutput, calls=%fused_computation.24 | convolution fusion | flops 805306368 | bytes 4718592
  218.5 0.4 convolution_bitcast_fusion.6
  219.0 0.3 copy.65
  219.3 0.3 reshape.65
  219.6 11.3 %all_to_all.21 = f32[32,1,1024]{2,1,0:T(1,128)S(1)} all-to-all(f32[32,1,1024]{2,1,0:T(1,128)S(1)} %reshape.65), channel_id=1, replica_groups=mesh['row'=4,'col'=8] {'row','col'}, dimensions={0} | all-to-all | bytes 262144 | tf_op jit(solution)/shard_map/all_to_all | solution.py:73
  230.9 0.9 reduce.2
  232.0 0.3 copy.43
  232.3 0.3 copy.44
  232.6 1.0 convolution_bitcast_fusion.1
  233.6 0.6 copy.46
  234.2 0.6 convolution_bitcast_fusion
  234.7 0.5 copy.47
  235.2 0.3 copy.48
  235.5 0.3 copy.49
  235.8 0.9 reshape.67
  236.7 2.6 all-to-all-start.3
  239.3 8.2 %shard_map.68 = (f32[1024,64]{1,0:T(8,128)}, f32[64,64]{1,0:T(8,128)}) custom-call(f32[1024,64]{1,0:T(8,128)} %all-reduce.2.cloned.1.call-done.image_ref), custom_call_target="tpu_custom_call" | custom-call | tf_op jit(solution)/shard_map/pallas_call | solution.py:42
  247.5 1.9 copy.51
  249.4 0.9 reduce.3
  250.6 0.3 copy.50
  251.0 1.8 fusion.6
  (21 shorter events, 1.5 us)
Async XLA Ops:
  7.2 5.5 %copy-start = (f32[1024,64]{0,1:T(8,128)S(1)}, f32[1024,64]{0,1:T(8,128)}, u32[]{:S(2)}) copy-start(f32[1024,64]{0,1:T(8,128)} %param.9) | copy-start | bytes 786436
  12.6 5.2 %copy-start.1 = (f32[32,16]{0,1:T(8,128)S(1)}, f32[32,16]{0,1:T(8,128)}, u32[]{:S(2)}) copy-start(f32[32,16]{0,1:T(8,128)} %param.8) | copy-start | bytes 6148
  12.6 14.4 %copy-start.2 = (f32[8,32]{1,0:T(8,128)S(1)}, f32[8,32]{1,0:T(8,128)}, u32[]{:S(2)}) copy-start(f32[8,32]{1,0:T(8,128)} %param.6) | copy-start | bytes 3076
  12.6 19.6 %copy-start.3 = (f32[4,32]{1,0:T(4,128)S(1)}, f32[4,32]{1,0:T(4,128)}, u32[]{:S(2)}) copy-start(f32[4,32]{1,0:T(4,128)} %param.7) | copy-start | bytes 1540
  19.7 39.1 %all-to-all-start = ((f32[32,1,1024]{2,1,0:T(1,128)}), f32[32,1,1024]{2,1,0:T(1,128)S(1)}, u32[]{:S(2)}, u32[]{:S(2)}) async-start(f32[32,1,1024]{2,1,0:T(1,128)} %reshape.61), calls=%async_computation | async-start | bytes 262144 | tf_op jit(solution)/shard_map/all_to_all | solution.py:73
  27.0 186.2 %all-reduce.2.cloned.1.call-start = ((), (), s32[]{:S(2)}) async-start(), calls=%async_computation.4 | async-start | bytes 1048576 | tf_op jit(solution)/shard_map/psum | solution.py:91
  236.7 12.7 %all-to-all-start.3 = ((f32[32,1,1024]{2,1,0:T(1,128)}), f32[32,1,1024]{2,1,0:T(1,128)S(1)}, u32[]{:S(2)}, u32[]{:S(2)}) async-start(f32[32,1,1024]{2,1,0:T(1,128)} %reshape.67), calls=%async_computation.3 | async-start | bytes 262144 | tf_op jit(solution)/shard_map/all_to_all | solution.py:81
Sparse Core Ops, SparseCore 0:
  86.3 126.8 all-reduce.1

commit v2 on v1

--- a/solution.py
+++ b/solution.py
@@ -1,3 +1,5 @@
+import functools
+
 import jax
 import jax.numpy as jnp
 from jax import lax
@@ -6,6 +8,7 @@
 from jax.sharding import PartitionSpec as P
 
 HIGHEST = lax.Precision.HIGHEST
+LANES = 128
 
 
 def dot(a, b, dims):
@@ -48,6 +51,94 @@
     )(image)
 
 
+def place():
+    return lax.axis_index("row") * lax.axis_size("col") + lax.axis_index("col")
+
+
+def greet(devices):
+    cols = lax.axis_size("col")
+    me = place()
+    barrier = pltpu.get_barrier_semaphore()
+
+    def hello(k, carry):
+        peer = lax.rem(me + k, devices)
+        pl.semaphore_signal(barrier, inc=1, device_id=(peer // cols, lax.rem(peer, cols)), device_id_type=pl.DeviceIdType.MESH)
+        return carry
+
+    lax.fori_loop(1, devices, hello, 0)
+    pl.semaphore_wait(barrier, devices - 1)
+
+
+def send_all(devices, source, target, send_sem, recv_sem):
+    cols = lax.axis_size("col")
+    me = place()
+
+    def send(k, carry):
+        peer = lax.rem(me + k, devices)
+        pltpu.make_async_remote_copy(
+            src_ref=source(peer),
+            dst_ref=target.at[me],
+            send_sem=send_sem,
+            recv_sem=recv_sem,
+            device_id=(peer // cols, lax.rem(peer, cols)),
+            device_id_type=pl.DeviceIdType.MESH,
+        ).start()
+        return carry
+
+    lax.fori_loop(1, devices, send, 0)
+    whole = target.at[pl.ds(0, devices - 1)]
+    pltpu.make_async_copy(whole, whole, send_sem).wait()
+    pltpu.make_async_copy(whole, whole, recv_sem).wait()
+
+
+def swap_kernel(devices, put_ref, out_ref, held, send_sem, recv_sem):
+    me = place()
+    greet(devices)
+    send_all(devices, lambda peer: put_ref.at[peer], held, send_sem, recv_sem)
+    held[me] = put_ref[me]
+    out_ref[...] = held[...]
+
+
+def total_kernel(devices, put_ref, out_ref, held, mine, spread, sems):
+    me = place()
+    greet(devices)
+    send_all(devices, lambda peer: put_ref.at[peer], held, sems.at[0], sems.at[1])
+    held[me] = put_ref[me]
+    mine[...] = jnp.sum(held[...], axis=0)
+    send_all(devices, lambda peer: mine, spread, sems.at[2], sems.at[3])
+    spread[me] = mine[...]
+    out_ref[...] = spread[...]
+
+
+def swap(values, ident):
+    devices = values.shape[0]
+    return pl.pallas_call(
+        functools.partial(swap_kernel, devices),
+        out_shape=jax.ShapeDtypeStruct(values.shape, jnp.float32),
+        in_specs=[pl.BlockSpec(memory_space=pltpu.VMEM)],
+        out_specs=pl.BlockSpec(memory_space=pltpu.VMEM),
+        scratch_shapes=[pltpu.VMEM(values.shape, jnp.float32), pltpu.SemaphoreType.DMA, pltpu.SemaphoreType.DMA],
+        compiler_params=pltpu.CompilerParams(collective_id=ident, has_side_effects=True),
+    )(values)
+
+
+def total(values, ident):
+    devices = values.shape[0]
+    return pl.pallas_call(
+        functools.partial(total_kernel, devices),
+        out_shape=jax.ShapeDtypeStruct(values.shape, jnp.float32),
+        in_specs=[pl.BlockSpec(memory_space=pltpu.VMEM)],
+        out_specs=pl.BlockSpec(memory_space=pltpu.VMEM),
+        scratch_shapes=[
+            pltpu.VMEM(values.shape, jnp.float32),
+            pltpu.VMEM(values.shape[1:], jnp.float32),
+            pltpu.VMEM(values.shape, jnp.float32),
+            pltpu.SemaphoreType.DMA((4,)),
+        ],
+        compiler_params=pltpu.CompilerParams(collective_id=ident, has_side_effects=True),
+    )(values)
+
+
 def shards(tensor, factor_two, factor_three, factor_four, factor_init):
     axes = ("row", "col")
     first_len, local_two, width = tensor.shape
@@ -60,40 +151,55 @@
     features = rank_four * rank_one
     part = features // devices
     data = tensor.reshape(first_len, local_pairs, fourth_len)
-    whole_two = lax.all_gather(factor_two, "row", axis=0, tiled=True)
-    whole_three = lax.all_gather(factor_three, "col", axis=0, tiled=True)
-    whole_two_len, rank_two = whole_two.shape
-    whole_three_len, rank_three = whole_three.shape
+    rank_two, rank_three = factor_two.shape[1], factor_three.shape[1]
 
     def pull(vectors):
         mixed = jnp.einsum("apd,ar->prd", data, vectors, precision=HIGHEST)
         return jnp.einsum("prd,de->per", mixed, factor_four, precision=HIGHEST).reshape(local_pairs, features)
 
-    def spread(block):
-        got = lax.all_to_all(block.reshape(local_pairs, devices, part).transpose(1, 0, 2), axes, 0, 0, tiled=True)
+    def share(values, ident):
+        length = values.shape[1]
+        padded = -(-length // LANES) * LANES
+        values = jnp.pad(values, ((0, 0), (0, padded - length))).reshape(devices, padded // LANES, LANES)
+        return swap(values, ident).reshape(devices, padded)[:, :length]
+
+    def spread(block, ident, extra=None):
+        put = block.reshape(local_pairs, devices, part).transpose(1, 0, 2).reshape(devices, local_pairs * part)
+        if extra is not None:
+            put = jnp.concatenate([put, jnp.broadcast_to(extra[None], (devices, extra.shape[0]))], axis=1)
+        got = share(put, ident)
+        rest = got[:, local_pairs * part:]
+        got = got[:, :local_pairs * part]
         got = got.reshape(rows, cols, local_two, local_three, part)
-        return got.transpose(0, 2, 1, 3, 4).reshape(rows * local_two, cols * local_three, part)
-
-    def gather(block):
+        return got.transpose(0, 2, 1, 3, 4).reshape(rows * local_two, cols * local_three, part), rest
+
+    def gather(block, ident):
         two, three, _ = block.shape
         put = block.reshape(rows, two // rows, cols, three // cols, part).transpose(0, 2, 1, 3, 4)
-        put = put.reshape(devices, (two // rows) * (three // cols), part)
-        got = lax.all_to_all(put, axes, 0, 0, tiled=True)
+        got = share(put.reshape(devices, -1), ident).reshape(devices, (two // rows) * (three // cols), part)
         return got.transpose(1, 0, 2).reshape(got.shape[1], features)
 
-    block = spread(pull(factor_init))
+    extra = jnp.concatenate([factor_two.reshape(-1), factor_three.reshape(-1)])
+    block, rest = spread(pull(factor_init), 1, extra)
+    rest = rest.reshape(rows, cols, -1)
+    whole_two = rest[:, 0, :factor_two.size].reshape(-1, rank_two)
+    whole_three = rest[0, :, factor_two.size:].reshape(-1, rank_three)
     block = jnp.einsum("bcq,bg->gcq", block, whole_two, precision=HIGHEST)
     block = jnp.einsum("gcq,cf->gfq", block, whole_three, precision=HIGHEST)
     block = jnp.einsum("gfq,cf->gcq", block, whole_three, precision=HIGHEST)
     block = jnp.einsum("gcq,bg->bcq", block, whole_two, precision=HIGHEST)
-    block = gather(block).reshape(local_pairs, rank_four, rank_one)
+    block = gather(block, 2).reshape(local_pairs, rank_four, rank_one)
     block = jnp.einsum("per,de->pdr", block, factor_four, precision=HIGHEST)
-    image = lax.psum(dot(tensor.reshape(first_len, -1), block.reshape(-1, rank_one), ((1,), (0,))), axes)
+    image = dot(tensor.reshape(first_len, -1), block.reshape(-1, rank_one), ((1,), (0,)))
+    half = first_len // 2
+    image = jnp.concatenate([image[:half], image[half:]], axis=1).reshape(devices, half // devices, 2 * rank_one)
+    image = total(image, 0).reshape(half, 2 * rank_one)
+    image = jnp.concatenate([image[:, :rank_one], image[:, rank_one:]], axis=0)
     basis, inverse = finish(image)
-    block = spread(pull(image))
+    block, _ = spread(pull(image), 3)
     block = jnp.einsum("bcq,bg->gcq", block, whole_two, precision=HIGHEST)
     block = jnp.einsum("gcq,cf->gfq", block, whole_three, precision=HIGHEST)
-    block = gather(block).reshape(-1, rank_four, rank_one)
+    block = gather(block, 4).reshape(-1, rank_four, rank_one)
     core = jnp.einsum("per,sr->spe", block, inverse, precision=HIGHEST)
     return (basis, core.reshape(rank_one, rank_two // rows, rank_three // cols, rank_four))
 

time: 260 us -> 123 us (0.47)
  waiting for transfers between devices: 127 us -> 0 us
  Pallas kernels: 8.18 us -> 72.9 us
  blocking collectives: 54.5 us -> 0 us
  between operations: 14.4 us -> 0.98 us
  starting transfers between devices: 9.95 us -> 0 us
  local copies, waits for them, and re-layouts: 17.5 us -> 22.1 us
  other arithmetic: 3.75 us -> 0.87 us
    psum x1 -> x0, waiting for transfers between devices: 127 us -> none  [shards(): lax.psum(dot(tensor.reshape(first_len, -1), block.reshape(-1, rank_one),...]
    pallas_call x0 -> x5, Pallas kernels: none -> 64.7 us  [the longest x4 43.4 us: swap(): pl.pallas_call(functools.partial(swap_kernel, devices), out_shape=jax.Sha...]
    all_gather x2 -> x0, blocking collectives: 31.7 us -> none  [the longest x1 26.5 us: shards(): whole_three = lax.all_gather(factor_three, 'col', axis=0, tiled=True)]
    all_to_all x2 -> x0, blocking collectives: 22.8 us -> none  [the longest x1 11.6 us: gather(): got = lax.all_to_all(put, axes, 0, 0, tiled=True)]
    all_to_all x2 -> x0, starting transfers between devices: 9.91 us -> none  [the longest x1 7.33 us: spread(): lax.all_to_all(block.reshape(local_pairs, devices, part).transpose(1, 0,...]
    reshape x2 -> x11, local copies, waits for them, and re-layouts: 0.62 us -> 5.65 us  [the longest x4 3.39 us: share(): jnp.pad(values, ((0, 0), (0, padded - length)))]
    all_to_all x4 -> x0, other arithmetic: 3.75 us -> none  [the longest x2 1.88 us: gather(): got = lax.all_to_all(put, axes, 0, 0, tiled=True)]
    another operation x1 -> x8, local copies, waits for them, and re-layouts: 0.13 us -> 3.71 us  [the longest x2 2.13 us: gather(): share(put.reshape(devices, -1), ident)]
  transfers between devices with their start and end apart: 3 -> 0, of which waited for: 1 -> 0; matrix products, arithmetic and copies ran while one was open for 1% -> 0% of each run, Pallas kernels for 3% -> 0%
where the time goes in v2:
time: 123 us
  Pallas kernels  72.9 us (59%)
  matrix products  25.7 us (21%)
  local copies, waits for them, and re-layouts  22.1 us (18%)
    pallas_call x4, Pallas kernels, swap(): pl.pallas_call(functools.partial(swap_kernel, devices), out_shape=jax.Sha...  43.4 us
    pallas_call x1, Pallas kernels, total(): pl.pallas_call(functools.partial(total_kernel, devices), out_shape=jax.Sh...  21.2 us
    unnamed x2, matrix products  10.4 us
    unnamed x9, local copies, waits for them, and re-layouts  8.38 us
    pallas_call x1, Pallas kernels, finish(): pl.pallas_call(finish_kernel, out_shape=(jax.ShapeDtypeStruct(image.shape...  8.18 us
    dot_general x1, matrix products, dot(): lax.dot_general(a, b, (dims, ((), ())), precision=HIGHEST, preferred_elem...  6.76 us
    reshape x4, local copies, waits for them, and re-layouts, share(): jnp.pad(values, ((0, 0), (0, padded - length)))  3.39 us
    dot_general x1, matrix products, shards(): block = jnp.einsum('gcq,bg->bcq', block, whole_two, precision=HIGHEST)  2.48 us

profile of v2, /device:TPU:0, one launch (start us, length us, event | category | flops | bytes accessed | tf_op | source)
XLA Modules:
  0.0 122.5 jit_solution(2868407637937328510)
XLA Ops:
  0.6 0.8 reshape.75
  1.5 0.8 reshape.74
  2.2 5.4 %copy.17 = f32[1024,8,128]{0,2,1:T(8,128)} copy(f32[1024,8,128]{2,1,0:T(8,128)} %param.5) | data formatting | bytes 8388608 | tf_op args[0]
  7.7 5.2 %fusion.21 = f32[64,1024]{0,1:S(1)} fusion(f32[1024,64]{0,1:T(8,128)S(1)} %copy-done, f32[1024,1024]{0,1:T(8,128)} %bitcast.94), kind=kOutput, calls=%fused_computation.32 | convolution fusion | flops 805306368 | bytes 4718592
  12.9 0.4 convolution_bitcast_fusion.3
  13.3 0.1 reshape_reshape.19
  13.4 0.3 copy.18
  13.8 0.2 reshape.73
  14.0 0.7 reshape.76.put_ref
  14.8 13.9 %shard_map.68 = f32[32,11,128]{2,1,0:T(8,128)} custom-call(f32[32,11,128]{2,1,0:T(8,128)} %reshape.76.put_ref), custom_call_target="tpu_custom_call" | custom-call | tf_op jit(solution)/shard_map/pallas_call | solution.py:115
  28.7 1.0 copy.53
  29.8 0.1 reshape.93
  30.1 0.3 reshape.79
  30.4 0.6 fusion.22
  31.0 0.9 convolution_bitcast_fusion.1
  31.9 0.6 fusion.23
  32.5 0.4 copy.20
  32.9 2.5 %convolution_bitcast_fusion = f32[4,8,8,4,32]{4,2,3,1,0:T(8,128)S(1)} fusion(f32[8,4,32,32]{3,2,1,0:T(8,128)S(1)} %copy.20, f32[4,8,32,1,1]{2,1,0,3,4:T(8,128)S(1)} %reshape.95), kind=kOutput, calls=%fused_computation.3 | convolution fusion | flops 12582912 | bytes 266240 | tf_op jit(solution)/shard_map/gcq,bg->bcq/dot_general | solution.py:190
  35.4 0.1 copy.21
  35.5 0.9 reshape.81.put_ref
  36.4 9.7 %shard_map.69 = f32[32,8,128]{2,1,0:T(8,128)} custom-call(f32[32,8,128]{2,1,0:T(8,128)} %reshape.81.put_ref), custom_call_target="tpu_custom_call" | custom-call | tf_op jit(solution)/shard_map/pallas_call | solution.py:115
  46.2 1.1 reshape_reshape.20
  47.3 0.3 copy.22
  47.6 0.1 reshape_reshape.21
  47.7 0.6 fusion.15
  48.3 6.8 %fusion.3 = f32[1024,64]{0,1:T(8,128)S(1)} fusion(f32[1024,64]{1,0:T(8,128)S(1)} %bitcast.99, f32[128,8,8,128]{3,2,1,0:T(8,128)} %bitcast.96), kind=kOutput, calls=%fused_computation.5 | convolution fusion | flops 805306368 | bytes 4718592 | tf_op jit(solution)/shard_map/dot_general | solution.py:15
  55.1 0.8 copy.23
  56.0 21.2 %shard_map.70 = f32[32,16,128]{2,1,0:T(8,128)} custom-call(f32[32,16,128]{2,1,0:T(8,128)} %bitcast.111), custom_call_target="tpu_custom_call" | custom-call | tf_op jit(solution)/shard_map/pallas_call | solution.py:127
  77.2 1.2 fusion.19
  78.4 5.2 %fusion.18 = f32[64,1024]{0,1:S(1)} fusion(f32[1024,1024]{0,1:T(8,128)} %bitcast.95, f32[512,64]{1,0:T(8,128)S(1)} %get-tuple-element.11, f32[512,64]{1,0:T(8,128)S(1)} %get-tuple-element.10), kind=kOutput, calls=%fused_computation.29 | convolution fusion | flops 805371904 | bytes 4718592
  83.6 0.8 pad_maximum_fusion.image_ref
  84.5 0.4 convolution_bitcast_fusion.2
  84.9 8.2 %shard_map.71 = (f32[1024,64]{1,0:T(8,128)}, f32[64,64]{1,0:T(8,128)}) custom-call(f32[1024,64]{1,0:T(8,128)} %pad_maximum_fusion.image_ref), custom_call_target="tpu_custom_call" | custom-call | tf_op jit(solution)/shard_map/pallas_call | solution.py:45
  93.0 1.9 %copy.29 = f32[1024,64]{0,1:T(8,128)} copy(f32[1024,64]{1,0:T(8,128)} %get-tuple-element.8) | data formatting | bytes 524288
  95.0 0.1 reshape_reshape.22
  95.1 0.3 copy.52
  95.4 0.8 reshape.86.put_ref
  96.3 10.3 %shard_map.72 = f32[32,8,128]{2,1,0:T(8,128)} custom-call(f32[32,8,128]{2,1,0:T(8,128)} %reshape.86.put_ref), custom_call_target="tpu_custom_call" | custom-call | tf_op jit(solution)/shard_map/pallas_call | solution.py:115
  106.6 1.2 reshape_reshape.23
  107.8 0.6 fusion.24
  108.5 0.9 fusion.7
  109.3 0.1 copy.51
  109.5 0.9 reshape.89.put_ref
  110.4 9.5 %shard_map.73 = f32[32,8,128]{2,1,0:T(8,128)} custom-call(f32[32,8,128]{2,1,0:T(8,128)} %reshape.89.put_ref), custom_call_target="tpu_custom_call" | custom-call | tf_op jit(solution)/shard_map/pallas_call | solution.py:115
  119.9 1.1 reshape_reshape.24
  121.0 0.3 copy.28
  121.3 0.1 dot_general.65
  121.4 1.1 fusion.10
  (19 shorter events, 0.4 us)
Async XLA Ops:
  0.6 7.0 %copy-start = (f32[1024,64]{0,1:T(8,128)S(1)}, f32[1024,64]{0,1:T(8,128)}, u32[]{:S(2)}) copy-start(f32[1024,64]{0,1:T(8,128)} %param.9) | copy-start | bytes 786436
  7.7 5.2 %copy-start.1 = (f32[32,16]{0,1:T(8,128)S(1)}, f32[32,16]{0,1:T(8,128)}, u32[]{:S(2)}) copy-start(f32[32,16]{0,1:T(8,128)} %param.8) | copy-start | bytes 6148
  106.6 14.9 %copy-start.2 = (f32[64,64]{1,0:T(8,128)S(1)}, f32[64,64]{1,0:T(8,128)}, u32[]{:S(2)}) copy-start(f32[64,64]{1,0:T(8,128)} %get-tuple-element.5) | copy-start | bytes 49156

commit v3 on v2

--- a/solution.py
+++ b/solution.py
@@ -154,7 +154,7 @@
     rank_two, rank_three = factor_two.shape[1], factor_three.shape[1]
 
     def pull(vectors):
-        mixed = jnp.einsum("apd,ar->prd", data, vectors, precision=HIGHEST)
+        mixed = jnp.einsum("apd,ar->prd", data, vectors, precision=lax.Precision.HIGH)
         return jnp.einsum("prd,de->per", mixed, factor_four, precision=HIGHEST).reshape(local_pairs, features)
 
     def share(values, ident):
@@ -190,7 +190,7 @@
     block = jnp.einsum("gcq,bg->bcq", block, whole_two, precision=HIGHEST)
     block = gather(block, 2).reshape(local_pairs, rank_four, rank_one)
     block = jnp.einsum("per,de->pdr", block, factor_four, precision=HIGHEST)
-    image = dot(tensor.reshape(first_len, -1), block.reshape(-1, rank_one), ((1,), (0,)))
+    image = jnp.dot(tensor.reshape(first_len, -1), block.reshape(-1, rank_one), precision=lax.Precision.HIGH)
     half = first_len // 2
     image = jnp.concatenate([image[:half], image[half:]], axis=1).reshape(devices, half // devices, 2 * rank_one)
     image = total(image, 0).reshape(half, 2 * rank_one)

time: 123 us -> 119 us (0.967)
  matrix products: 25.7 us -> 21.3 us
    unnamed x2, matrix products: 10.4 us -> 8 us
    dot_general x1, matrix products: 6.76 us -> 4.73 us  [shards(): jnp.dot(tensor.reshape(first_len, -1), block.reshape(-1, rank_one), preci...]
where the time goes in v3:
time: 119 us; the launch traced here: 118 us
  Pallas kernels  72.9 us (61%)
  local copies, waits for them, and re-layouts  22.1 us (19%)
  matrix products  21.3 us (18%)
    pallas_call x4, Pallas kernels, swap(): pl.pallas_call(functools.partial(swap_kernel, devices), out_shape=jax.Sha...  43.5 us
    pallas_call x1, Pallas kernels, total(): pl.pallas_call(functools.partial(total_kernel, devices), out_shape=jax.Sh...  21.2 us
    unnamed x9, local copies, waits for them, and re-layouts  8.38 us
    pallas_call x1, Pallas kernels, finish(): pl.pallas_call(finish_kernel, out_shape=(jax.ShapeDtypeStruct(image.shape...  8.18 us
    unnamed x2, matrix products  8 us
    dot_general x1, matrix products, shards(): jnp.dot(tensor.reshape(first_len, -1), block.reshape(-1, rank_one), preci...  4.73 us
    reshape x4, local copies, waits for them, and re-layouts, share(): jnp.pad(values, ((0, 0), (0, padded - length)))  3.39 us
    dot_general x1, matrix products, shards(): block = jnp.einsum('gcq,bg->bcq', block, whole_two, precision=HIGHEST)  2.48 us

profile of v3, /device:TPU:0, one launch (start us, length us, event | category | flops | bytes accessed | tf_op | source)
XLA Modules:
  0.0 118.0 jit_solution(10538729618314387405)
XLA Ops:
  0.6 0.8 reshape.75
  1.5 0.8 reshape.74
  2.2 5.4 %copy.17 = f32[1024,8,128]{0,2,1:T(8,128)} copy(f32[1024,8,128]{2,1,0:T(8,128)} %param.5) | data formatting | bytes 8388608 | tf_op args[0]
  7.7 4.0 %fusion.21 = f32[64,1024]{0,1:S(1)} fusion(f32[1024,64]{0,1:T(8,128)S(1)} %copy-done, f32[1024,1024]{0,1:T(8,128)} %bitcast.94), kind=kOutput, calls=%fused_computation.32 | convolution fusion | flops 402653184 | bytes 4718592
  11.7 0.4 convolution_bitcast_fusion.3
  12.1 0.1 reshape_reshape.19
  12.2 0.3 copy.18
  12.5 0.2 reshape.73
  12.8 0.7 reshape.76.put_ref
  13.5 13.9 %shard_map.68 = f32[32,11,128]{2,1,0:T(8,128)} custom-call(f32[32,11,128]{2,1,0:T(8,128)} %reshape.76.put_ref), custom_call_target="tpu_custom_call" | custom-call | tf_op jit(solution)/shard_map/pallas_call | solution.py:115
  27.5 1.0 copy.53
  28.5 0.1 reshape.93
  28.8 0.3 reshape.79
  29.2 0.6 fusion.22
  29.8 0.9 convolution_bitcast_fusion.1
  30.7 0.6 fusion.23
  31.3 0.4 copy.20
  31.7 2.5 %convolution_bitcast_fusion = f32[4,8,8,4,32]{4,2,3,1,0:T(8,128)S(1)} fusion(f32[8,4,32,32]{3,2,1,0:T(8,128)S(1)} %copy.20, f32[4,8,32,1,1]{2,1,0,3,4:T(8,128)S(1)} %reshape.95), kind=kOutput, calls=%fused_computation.3 | convolution fusion | flops 12582912 | bytes 266240 | tf_op jit(solution)/shard_map/gcq,bg->bcq/dot_general | solution.py:190
  34.2 0.1 copy.21
  34.3 0.9 reshape.81.put_ref
  35.2 9.7 %shard_map.69 = f32[32,8,128]{2,1,0:T(8,128)} custom-call(f32[32,8,128]{2,1,0:T(8,128)} %reshape.81.put_ref), custom_call_target="tpu_custom_call" | custom-call | tf_op jit(solution)/shard_map/pallas_call | solution.py:115
  45.0 1.1 reshape_reshape.20
  46.0 0.3 copy.22
  46.4 0.1 reshape_reshape.21
  46.5 0.6 fusion.15
  47.1 4.7 %fusion.3 = f32[1024,64]{0,1:T(8,128)S(1)} fusion(f32[1024,64]{1,0:T(8,128)S(1)} %bitcast.99, f32[128,8,8,128]{3,2,1,0:T(8,128)} %bitcast.96), kind=kOutput, calls=%fused_computation.5 | convolution fusion | flops 402653184 | bytes 4718592 | tf_op jit(solution)/shard_map/dot_general | solution.py:193
  51.9 0.8 copy.23
  52.7 21.2 %shard_map.70 = f32[32,16,128]{2,1,0:T(8,128)} custom-call(f32[32,16,128]{2,1,0:T(8,128)} %bitcast.111), custom_call_target="tpu_custom_call" | custom-call | tf_op jit(solution)/shard_map/pallas_call | solution.py:127
  74.0 1.2 fusion.19
  75.1 4.0 %fusion.18 = f32[64,1024]{0,1:S(1)} fusion(f32[1024,1024]{0,1:T(8,128)} %bitcast.95, f32[512,64]{1,0:T(8,128)S(1)} %get-tuple-element.11, f32[512,64]{1,0:T(8,128)S(1)} %get-tuple-element.10), kind=kOutput, calls=%fused_computation.29 | convolution fusion | flops 402718720 | bytes 4718592
  79.2 0.8 pad_maximum_fusion.image_ref
  80.0 0.4 convolution_bitcast_fusion.2
  80.4 8.2 %shard_map.71 = (f32[1024,64]{1,0:T(8,128)}, f32[64,64]{1,0:T(8,128)}) custom-call(f32[1024,64]{1,0:T(8,128)} %pad_maximum_fusion.image_ref), custom_call_target="tpu_custom_call" | custom-call | tf_op jit(solution)/shard_map/pallas_call | solution.py:45
  88.6 1.9 %copy.29 = f32[1024,64]{0,1:T(8,128)} copy(f32[1024,64]{1,0:T(8,128)} %get-tuple-element.8) | data formatting | bytes 524288
  90.5 0.1 reshape_reshape.22
  90.7 0.3 copy.52
  91.0 0.8 reshape.86.put_ref
  91.8 10.3 %shard_map.72 = f32[32,8,128]{2,1,0:T(8,128)} custom-call(f32[32,8,128]{2,1,0:T(8,128)} %reshape.86.put_ref), custom_call_target="tpu_custom_call" | custom-call | tf_op jit(solution)/shard_map/pallas_call | solution.py:115
  102.1 1.2 reshape_reshape.23
  103.4 0.6 fusion.24
  104.0 0.9 fusion.7
  104.9 0.1 copy.51
  105.0 0.9 reshape.89.put_ref
  105.9 9.5 %shard_map.73 = f32[32,8,128]{2,1,0:T(8,128)} custom-call(f32[32,8,128]{2,1,0:T(8,128)} %reshape.89.put_ref), custom_call_target="tpu_custom_call" | custom-call | tf_op jit(solution)/shard_map/pallas_call | solution.py:115
  115.4 1.1 reshape_reshape.24
  116.5 0.3 copy.28
  116.8 0.1 dot_general.65
  117.0 1.1 fusion.10
  (19 shorter events, 0.4 us)
Async XLA Ops:
  0.6 7.0 %copy-start = (f32[1024,64]{0,1:T(8,128)S(1)}, f32[1024,64]{0,1:T(8,128)}, u32[]{:S(2)}) copy-start(f32[1024,64]{0,1:T(8,128)} %param.9) | copy-start | bytes 786436
  7.7 4.0 %copy-start.1 = (f32[32,16]{0,1:T(8,128)S(1)}, f32[32,16]{0,1:T(8,128)}, u32[]{:S(2)}) copy-start(f32[32,16]{0,1:T(8,128)} %param.8) | copy-start | bytes 6148
  102.1 14.9 %copy-start.2 = (f32[64,64]{1,0:T(8,128)S(1)}, f32[64,64]{1,0:T(8,128)}, u32[]{:S(2)}) copy-start(f32[64,64]{1,0:T(8,128)} %get-tuple-element.5) | copy-start | bytes 49156
